TPU v7x, 32 devices: a whole 2x2x4 slice. The times are simulated.
32 devices in a mesh: seq: 8 (over z, core), head: 4 (over y, x).
Axes of the slice: x: 2, y: 2, z: 4, core: 2. Of those that a mesh axis runs over, the one named last changes fastest.
Arguments:
- queries: bfloat16 [1024, 2048], P('seq', 'head'), may hold values from -192 to 192
- keys: bfloat16 [1024, 512], P('seq', 'head'), may hold values from -5 to 5
- values: bfloat16 [1024, 512], P('seq', 'head'), may hold values from -24 to 24
- segments: int32 [1024], replicated, may hold values from 0 to 5, never falling along the last dimension, each value on 1 to 341 neighbouring positions
- out_weight: bfloat16 [2048, 8192], P(None, 'head'), may hold values from -0.125 to 0.125
Outputs:
- mixed: bfloat16 [1024, 8192], P('seq', 'head')
All inputs are finite; a program needn't handle non-finite values.
Results may differ from a plain program's by a relative error of at most 0.007.
Values may be sent and summed in bfloat16 or wider, within the bound.
A program may use at most 64 MiB of HBM per device.

v0:
```python
import jax
import jax.numpy as jnp
from jax import lax
from jax.sharding import PartitionSpec as P

HD = 128
WIN_BLK = 31
masked_score = -1e30


def passed_along(block, axis, distance):
    devices = range(lax.axis_size(axis))
    route = [(i - distance, i) for i in devices if i - distance in devices]
    return lax.ppermute(block, axis, route)


def allowed_keys(segments, query_pos, query_seg, key_first, key_count, window_len):
    key_pos = key_first + jnp.arange(key_count, dtype=jnp.int32)
    clipped = jnp.clip(key_pos, 0, segments.shape[0] - 1)
    key_seg = jnp.take(segments, clipped)
    allowed = key_pos[None, :] <= query_pos[:, None]
    allowed = allowed & (query_pos[:, None] - key_pos[None, :] < window_len)
    allowed = allowed & (key_pos[None, :] >= 0)
    return allowed & (key_seg[None, :] == query_seg[:, None])


def absorb(carry_state, query_heads, key_piece, value_piece, allowed):
    row_max, row_sum, accum = carry_state
    key_count = key_piece.shape[0]
    kv_heads = query_heads.shape[1]
    key_heads = key_piece.reshape(key_count, kv_heads, HD)
    value_heads = value_piece.reshape(key_count, kv_heads, HD)
    scores = jnp.einsum(
        "tagd,sad->agts", query_heads, key_heads, preferred_element_type=jnp.float32
    )
    scores = jnp.where(allowed[None, None], scores * HD ** (-0.5), masked_score)
    new_max = jnp.maximum(row_max, jnp.max(scores, axis=-1))
    weights = jnp.exp(scores - new_max[..., None])
    factor = jnp.exp(row_max - new_max)
    new_sum = row_sum * factor + jnp.sum(weights, axis=-1)
    update = jnp.einsum(
        "agts,sad->agtd",
        weights.astype(jnp.bfloat16),
        value_heads,
        preferred_element_type=jnp.float32,
    )
    return (new_max, new_sum, accum * factor[..., None] + update)


def on_device(queries, keys, values, segments, out_weight):
    row_count = queries.shape[0]
    kv_width = keys.shape[1]
    kv_heads = kv_width // HD
    group_size = queries.shape[1] // kv_width
    cycle_size = lax.axis_size("seq")
    position = lax.axis_index("seq")
    window_len = WIN_BLK * row_count
    reach_blocks = min(WIN_BLK, cycle_size - 1)
    own_first = position * row_count
    query_pos = own_first + jnp.arange(row_count, dtype=jnp.int32)
    query_seg = lax.dynamic_slice_in_dim(segments, own_first, row_count, 0)
    query_heads = queries.reshape(row_count, kv_heads, group_size, HD)
    start_state = (
        jnp.full((kv_heads, group_size, row_count), masked_score, jnp.float32),
        jnp.zeros((kv_heads, group_size, row_count), jnp.float32),
        jnp.zeros((kv_heads, group_size, row_count, HD), jnp.float32),
    )

    def take_block(carry_state, key_piece, value_piece, key_first):
        allowed = allowed_keys(
            segments, query_pos, query_seg, key_first, key_piece.shape[0], window_len
        )
        return absorb(carry_state, query_heads, key_piece, value_piece, allowed)

    carry_state = take_block(start_state, keys, values, own_first)
    near_keys, near_values = passed_along((keys, values), "seq", 1)
    carry_state = take_block(carry_state, near_keys, near_values, own_first - row_count)
    pair_keys = jnp.concatenate([near_keys, keys], axis=0)
    pair_values = jnp.concatenate([near_values, values], axis=0)

    def pair_turn(turn_index, loop_carry):
        moving_keys, moving_values, inner_state = loop_carry
        moving_keys, moving_values = passed_along((moving_keys, moving_values), "seq", 2)
        key_first = own_first - (2 * turn_index + 3) * row_count
        inner_state = take_block(inner_state, moving_keys, moving_values, key_first)
        return (moving_keys, moving_values, inner_state)

    finished = lax.fori_loop(0, reach_blocks // 2, pair_turn, (pair_keys, pair_values, carry_state))
    carry_state = finished[2]
    row_max, row_sum, accum = carry_state
    attended = (accum / row_sum[..., None]).transpose(2, 0, 1, 3)
    attended = attended.reshape(row_count, queries.shape[1]).astype(jnp.bfloat16)
    mixed = jnp.dot(
        lax.all_gather(attended, "head", axis=1, tiled=True),
        out_weight,
        preferred_element_type=jnp.float32,
    )
    return mixed.astype(jnp.bfloat16)


def solution(mesh):
    return jax.shard_map(
        on_device,
        mesh=mesh,
        in_specs=(P("seq", "head"), P("seq", "head"), P("seq", "head"), P(), P(None, "head")),
        out_specs=P("seq", "head"),
        check_vma=False,
    )
```

profile of v0, /device:TPU:0, one launch (start us, length us, event | category | flops | bytes accessed | tf_op | source)
XLA Modules:
  0.0 60.8 jit_solution(18168356742073294899)
XLA Ops:
  0.0 2.4 %collective-permute-start.2 = (bf16[128,128]{1,0:T(8,128)(2,1)}, bf16[128,128]{1,0:T(8,128)(2,1)S(1)}, u32[]{:S(2)}, u32[]{:S(2)}) collective-permute-start(bf16[128,128]{1,0:T(8,128)(2,1)} %param.10), channel_id=1, source_target_pairs={{0,4},{4,8},{8,12},{12,16},{16,20},{20,24},{24,28},{1,5},{5,9},{9,... | collective-permute-start | bytes 98312 | tf_op jit(solution)/shard_map/ppermute | solution.py:14
  2.4 4.6 %collective-permute-start.3 = (bf16[128,128]{1,0:T(8,128)(2,1)}, bf16[128,128]{1,0:T(8,128)(2,1)S(1)}, u32[]{:S(2)}, u32[]{:S(2)}) collective-permute-start(bf16[128,128]{1,0:T(8,128)(2,1)} %param.11), channel_id=1, source_target_pairs={{0,4},{4,8},{8,12},{12,16},{16,20},{20,24},{24,28},{1,5},{5,9},{9,... | collective-permute-start | bytes 98312 | tf_op jit(solution)/shard_map/ppermute | solution.py:14
  7.1 0.8 %dynamic_slice.3 = s32[128]{0:T(128)S(1)} dynamic-slice(s32[1024]{0:T(1024)} %param.12, s32[]{:T(128)S(6)} %select_n.63), dynamic_slice_sizes={128} | dynamic-slice | bytes 1028 | tf_op jit(solution)/shard_map/dynamic_slice | solution.py:61
  7.8 1.6 %gather_fusion.2 = s32[128]{0:T(128)S(1)} fusion(s32[1024]{0:T(1024)} %param.12, s32[1024]{0:T(1024)S(1)} %pad_clamp_fusion.1), kind=kCustom, calls=%fused_computation.2.clone | custom fusion | bytes 1536 | tf_op jit(solution)/shard_map/jit(_take)/gather | solution.py:20
  9.5 1.6 %gather_fusion.1 = s32[128]{0:T(128)S(1)} fusion(s32[1024]{0:T(1024)} %param.12, s32[1024]{0:T(1024)S(1)} %pad_clamp_fusion.2), kind=kCustom, calls=%fused_computation.clone | custom fusion | bytes 1536 | tf_op jit(solution)/shard_map/jit(_take)/gather | solution.py:20
  11.1 0.2 fusion.40
  11.3 1.1 %fusion.54 = (f32[4,128]{1,0:T(4,128)S(1)}, f32[1,4,128,128]{2,3,1,0:T(8,128)S(1)}) fusion(bf16[128,128]{1,0:T(8,128)(2,1)} %param.10, pred[128,128]{0,1:T(8,128)(4,1)S(1)} %get-tuple-element.284, bf16[128,512]{1,0:T(8,128)(2,1)} %param.9), kind=kOutput, calls=%fused_computation.96 | convolution fusion | flops 16973312 | bytes 444416 | tf_op jit(solution)/shard_map/tagd,sad->agts/dot_general | solution.py:33
  12.4 1.0 %copy.16 = bf16[128,512]{0,1:T(8,128)(2,1)S(1)} copy(bf16[128,512]{1,0:T(8,128)(2,1)} %param.9) | data formatting | bytes 262144 | tf_op args[0]
  13.4 0.1 copy.17
  13.6 0.0 collective-permute-done.2
  13.6 1.1 %fusion.55 = (f32[4,128]{1,0:T(4,128)S(1)}, f32[1,4,128,128]{2,3,1,0:T(8,128)S(1)}) fusion(bf16[128,128]{1,0:T(8,128)(2,1)S(1)} %collective-permute-done.2, pred[128,128]{0,1:T(8,128)(4,1)S(1)} %get-tuple-element.285, bf16[128,512]{1,0:T(8,128)(2,1)} %param.9), kind=kOutput, calls=%fused_computation.97 | convolution fusion | flops 16973312 | bytes 444416 | tf_op jit(solution)/shard_map/tagd,sad->agts/dot_general | solution.py:33
  14.7 0.1 fusion.25
  14.8 1.0 %fusion.19 = f32[4,128,128]{2,1,0:T(8,128)S(1)} fusion(f32[1,4,128,128]{2,3,1,0:T(8,128)S(1)} %get-tuple-element.287, f32[4,128]{1,0:T(4,128)S(1)} %get-tuple-element.278, f32[4,128]{1,0:T(4,128)S(1)} %get-tuple-element.282, f32[4,128]{1,0:T(4,128)S(1)} %get-tuple-element.283, bf16[128,128]{1,0:T(8,128)(2,1)} %param.11), kind=kOutput, calls=%fused_computation.36 | convolution fusion | flops 17039360 | bytes 563200 | tf_op jit(solution)/shard_map/agts,sad->agtd/dot_general | solution.py:41
  15.8 0.1 fusion.27
  15.9 0.8 %pad_maximum_fusion = bf16[256,128]{1,0:T(8,128)(2,1)S(1)} fusion(bf16[128,128]{1,0:T(8,128)(2,1)} %param.10, bf16[128,128]{1,0:T(8,128)(2,1)S(1)} %collective-permute-done.2), kind=kLoop, calls=%fused_computation.58 | loop fusion | flops 131072 | bytes 131072 | tf_op jit(solution)/shard_map/concatenate | solution.py:78
  16.6 0.0 collective-permute-done.3
  16.6 0.8 %pad_maximum_fusion.1 = bf16[256,128]{1,0:T(8,128)(2,1)S(1)} fusion(bf16[128,128]{1,0:T(8,128)(2,1)} %param.11, bf16[128,128]{1,0:T(8,128)(2,1)S(1)} %collective-permute-done.3), kind=kLoop, calls=%fused_computation.59 | loop fusion | flops 131072 | bytes 131072 | tf_op jit(solution)/shard_map/concatenate | solution.py:79
  17.4 0.2 fusion.18
  17.6 26.8 %while.23 = (s32[]{:T(128)}, bf16[256,128]{1,0:T(8,128)(2,1)S(1)}, bf16[256,128]{1,0:T(8,128)(2,1)S(1)}, f32[1,4,128]{2,1,0:T(4,128)S(1)}, f32[1,4,128]{2,1,0:T(...) while((s32[]{:T(128)}, bf16[256,128]{1,0:T(8,128)(2,1)S(1)}, ...), condition=%wide.region_7.9_spmd.clone.clone, body=%wide.region_4.8_spmd.clone.clone.sunk | while | flops 68393600 | bytes 3260693 | solution.py:88
  17.6 3.5 %collective-permute-start = (bf16[256,128]{1,0:T(8,128)(2,1)S(1)}, bf16[256,128]{1,0:T(8,128)(2,1)S(1)}, u32[]{:S(2)}, u32[]{:S(2)}) collective-permute-start(bf16[256,128]{1,0:T(8,128)(2,1)S(1)} %get-tuple-element.384), channel_id=1, source_target_pairs={{0,8},{4,12},{8,16},{12,20},{16,24},{20,28},{1,9},{5,13},{9,17},{1... | collective-permute-start | bytes 196616 | tf_op jit(solution)/shard_map/while/body/eval_jaxpr/ppermute | solution.py:14
  21.1 3.5 %collective-permute-start.1 = (bf16[256,128]{1,0:T(8,128)(2,1)S(1)}, bf16[256,128]{1,0:T(8,128)(2,1)S(1)}, u32[]{:S(2)}, u32[]{:S(2)}) collective-permute-start(bf16[256,128]{1,0:T(8,128)(2,1)S(1)} %get-tuple-element.385), channel_id=1, source_target_pairs={{0,8},{4,12},{8,16},{12,20},{16,24},{20,28},{1,9},{5,13},{9,17},{1... | collective-permute-start | bytes 196616 | tf_op jit(solution)/shard_map/while/body/eval_jaxpr/ppermute | solution.py:14
  24.7 1.9 %gather_fusion = s32[256]{0:T(256)S(1)} fusion(s32[1024]{0:T(1024)} %get-tuple-element.404, s32[1024]{0:T(1024)S(1)} %pad_clamp_fusion.4), kind=kCustom, calls=%fused_computation.1.clone.clone.clone.1 | custom fusion | bytes 3072 | tf_op jit(solution)/shard_map/while/body/eval_jaxpr/jit(_take)/gather | solution.py:20
  26.6 0.2 fusion.71
  26.8 0.0 collective-permute-done
  26.8 0.2 fusion.72
  27.1 0.1 fusion.74
  27.2 0.0 collective-permute-done.1
  27.3 0.3 fusion.75
  27.6 3.5 %collective-permute-start = (bf16[256,128]{1,0:T(8,128)(2,1)S(1)}, bf16[256,128]{1,0:T(8,128)(2,1)S(1)}, u32[]{:S(2)}, u32[]{:S(2)}) collective-permute-start(bf16[256,128]{1,0:T(8,128)(2,1)S(1)} %get-tuple-element.384), channel_id=1, source_target_pairs={{0,8},{4,12},{8,16},{12,20},{16,24},{20,28},{1,9},{5,13},{9,17},{1... | collective-permute-start | bytes 196616 | tf_op jit(solution)/shard_map/while/body/eval_jaxpr/ppermute | solution.py:14
  31.1 1.9 %collective-permute-start.1 = (bf16[256,128]{1,0:T(8,128)(2,1)S(1)}, bf16[256,128]{1,0:T(8,128)(2,1)S(1)}, u32[]{:S(2)}, u32[]{:S(2)}) collective-permute-start(bf16[256,128]{1,0:T(8,128)(2,1)S(1)} %get-tuple-element.385), channel_id=1, source_target_pairs={{0,8},{4,12},{8,16},{12,20},{16,24},{20,28},{1,9},{5,13},{9,17},{1... | collective-permute-start | bytes 196616 | tf_op jit(solution)/shard_map/while/body/eval_jaxpr/ppermute | solution.py:14
  33.1 1.9 %gather_fusion = s32[256]{0:T(256)S(1)} fusion(s32[1024]{0:T(1024)} %get-tuple-element.404, s32[1024]{0:T(1024)S(1)} %pad_clamp_fusion.4), kind=kCustom, calls=%fused_computation.1.clone.clone.clone.1 | custom fusion | bytes 3072 | tf_op jit(solution)/shard_map/while/body/eval_jaxpr/jit(_take)/gather | solution.py:20
  35.1 0.2 fusion.71
  35.3 0.0 collective-permute-done
  35.3 0.2 fusion.72
  35.5 0.1 fusion.74
  35.7 0.3 fusion.75
  36.0 3.5 %collective-permute-start = (bf16[256,128]{1,0:T(8,128)(2,1)S(1)}, bf16[256,128]{1,0:T(8,128)(2,1)S(1)}, u32[]{:S(2)}, u32[]{:S(2)}) collective-permute-start(bf16[256,128]{1,0:T(8,128)(2,1)S(1)} %get-tuple-element.384), channel_id=1, source_target_pairs={{0,8},{4,12},{8,16},{12,20},{16,24},{20,28},{1,9},{5,13},{9,17},{1... | collective-permute-start | bytes 196616 | tf_op jit(solution)/shard_map/while/body/eval_jaxpr/ppermute | solution.py:14
  39.6 1.9 %collective-permute-start.1 = (bf16[256,128]{1,0:T(8,128)(2,1)S(1)}, bf16[256,128]{1,0:T(8,128)(2,1)S(1)}, u32[]{:S(2)}, u32[]{:S(2)}) collective-permute-start(bf16[256,128]{1,0:T(8,128)(2,1)S(1)} %get-tuple-element.385), channel_id=1, source_target_pairs={{0,8},{4,12},{8,16},{12,20},{16,24},{20,28},{1,9},{5,13},{9,17},{1... | collective-permute-start | bytes 196616 | tf_op jit(solution)/shard_map/while/body/eval_jaxpr/ppermute | solution.py:14
  41.6 1.9 %gather_fusion = s32[256]{0:T(256)S(1)} fusion(s32[1024]{0:T(1024)} %get-tuple-element.404, s32[1024]{0:T(1024)S(1)} %pad_clamp_fusion.4), kind=kCustom, calls=%fused_computation.1.clone.clone.clone.1 | custom fusion | bytes 3072 | tf_op jit(solution)/shard_map/while/body/eval_jaxpr/jit(_take)/gather | solution.py:20
  43.5 0.2 fusion.71
  43.7 0.0 collective-permute-done
  43.7 0.2 fusion.72
  44.0 0.1 fusion.74
  44.1 0.0 collective-permute-done.1
  44.1 0.3 fusion.75
  44.5 0.1 copy.18
  44.7 10.7 %all_gather.3 = bf16[128,2048]{0,1:T(8,128)(2,1)S(1)} all-gather(bf16[128,512]{0,1:T(8,128)(2,1)S(1)} %bitcast.142), channel_id=1, replica_groups=mesh['seq'=8,'head'=4] {'head'}, dimensions={1}, use_global_device_ids=true | all-gather | bytes 655360 | tf_op jit(solution)/shard_map/all_gather | solution.py:94
  55.3 5.5 %convolution_convert_fusion = bf16[128,2048]{1,0:T(8,128)(2,1)} fusion(bf16[128,2048]{0,1:T(8,128)(2,1)S(1)} %all_gather.3, bf16[2048,2048]{1,0:T(8,128)(2,1)} %param.13), kind=kOutput, calls=%fused_computation.32 | convolution fusion | flops 1074003968 | bytes 9437184 | tf_op jit(solution)/shard_map/dot_general | solution.py:93
  (41 shorter events, 0.3 us)
Async XLA Ops:
  0.0 13.6 %collective-permute-start.2 = (bf16[128,128]{1,0:T(8,128)(2,1)}, bf16[128,128]{1,0:T(8,128)(2,1)S(1)}, u32[]{:S(2)}, u32[]{:S(2)}) collective-permute-start(bf16[128,128]{1,0:T(8,128)(2,1)} %param.10), channel_id=1, source_target_pairs={{0,4},{4,8},{8,12},{12,16},{16,20},{20,24},{24,28},{1,5},{5,9},{9,... | collective-permute-start | bytes 98312 | tf_op jit(solution)/shard_map/ppermute | solution.py:14
  2.4 14.2 %collective-permute-start.3 = (bf16[128,128]{1,0:T(8,128)(2,1)}, bf16[128,128]{1,0:T(8,128)(2,1)S(1)}, u32[]{:S(2)}, u32[]{:S(2)}) collective-permute-start(bf16[128,128]{1,0:T(8,128)(2,1)} %param.11), channel_id=1, source_target_pairs={{0,4},{4,8},{8,12},{12,16},{16,20},{20,24},{24,28},{1,5},{5,9},{9,... | collective-permute-start | bytes 98312 | tf_op jit(solution)/shard_map/ppermute | solution.py:14
  17.6 9.2 %collective-permute-start = (bf16[256,128]{1,0:T(8,128)(2,1)S(1)}, bf16[256,128]{1,0:T(8,128)(2,1)S(1)}, u32[]{:S(2)}, u32[]{:S(2)}) collective-permute-start(bf16[256,128]{1,0:T(8,128)(2,1)S(1)} %get-tuple-element.384), channel_id=1, source_target_pairs={{0,8},{4,12},{8,16},{12,20},{16,24},{20,28},{1,9},{5,13},{9,17},{1... | collective-permute-start | bytes 196616 | tf_op jit(solution)/shard_map/while/body/eval_jaxpr/ppermute | solution.py:14
  21.1 6.1 %collective-permute-start.1 = (bf16[256,128]{1,0:T(8,128)(2,1)S(1)}, bf16[256,128]{1,0:T(8,128)(2,1)S(1)}, u32[]{:S(2)}, u32[]{:S(2)}) collective-permute-start(bf16[256,128]{1,0:T(8,128)(2,1)S(1)} %get-tuple-element.385), channel_id=1, source_target_pairs={{0,8},{4,12},{8,16},{12,20},{16,24},{20,28},{1,9},{5,13},{9,17},{1... | collective-permute-start | bytes 196616 | tf_op jit(solution)/shard_map/while/body/eval_jaxpr/ppermute | solution.py:14
  27.6 7.7 %collective-permute-start = (bf16[256,128]{1,0:T(8,128)(2,1)S(1)}, bf16[256,128]{1,0:T(8,128)(2,1)S(1)}, u32[]{:S(2)}, u32[]{:S(2)}) collective-permute-start(bf16[256,128]{1,0:T(8,128)(2,1)S(1)} %get-tuple-element.384), channel_id=1, source_target_pairs={{0,8},{4,12},{8,16},{12,20},{16,24},{20,28},{1,9},{5,13},{9,17},{1... | collective-permute-start | bytes 196616 | tf_op jit(solution)/shard_map/while/body/eval_jaxpr/ppermute | solution.py:14
  31.1 4.5 %collective-permute-start.1 = (bf16[256,128]{1,0:T(8,128)(2,1)S(1)}, bf16[256,128]{1,0:T(8,128)(2,1)S(1)}, u32[]{:S(2)}, u32[]{:S(2)}) collective-permute-start(bf16[256,128]{1,0:T(8,128)(2,1)S(1)} %get-tuple-element.385), channel_id=1, source_target_pairs={{0,8},{4,12},{8,16},{12,20},{16,24},{20,28},{1,9},{5,13},{9,17},{1... | collective-permute-start | bytes 196616 | tf_op jit(solution)/shard_map/while/body/eval_jaxpr/ppermute | solution.py:14
  36.0 7.7 %collective-permute-start = (bf16[256,128]{1,0:T(8,128)(2,1)S(1)}, bf16[256,128]{1,0:T(8,128)(2,1)S(1)}, u32[]{:S(2)}, u32[]{:S(2)}) collective-permute-start(bf16[256,128]{1,0:T(8,128)(2,1)S(1)} %get-tuple-element.384), channel_id=1, source_target_pairs={{0,8},{4,12},{8,16},{12,20},{16,24},{20,28},{1,9},{5,13},{9,17},{1... | collective-permute-start | bytes 196616 | tf_op jit(solution)/shard_map/while/body/eval_jaxpr/ppermute | solution.py:14
  39.6 4.6 %collective-permute-start.1 = (bf16[256,128]{1,0:T(8,128)(2,1)S(1)}, bf16[256,128]{1,0:T(8,128)(2,1)S(1)}, u32[]{:S(2)}, u32[]{:S(2)}) collective-permute-start(bf16[256,128]{1,0:T(8,128)(2,1)S(1)} %get-tuple-element.385), channel_id=1, source_target_pairs={{0,8},{4,12},{8,16},{12,20},{16,24},{20,28},{1,9},{5,13},{9,17},{1... | collective-permute-start | bytes 196616 | tf_op jit(solution)/shard_map/while/body/eval_jaxpr/ppermute | solution.py:14
where the time goes:
time: 61.6 us; the launch traced here: 60.8 us
  starting transfers between devices  24.9 us (40%)
  local copies, waits for them, and re-layouts  11.1 us (18%)
  blocking collectives  10.7 us (17%)
  matrix products  10.6 us (17%)
  other arithmetic  2.91 us (5%)
    ppermute x8, starting transfers between devices, passed_along(): return lax.ppermute(block, axis, route)  24.9 us
    all_gather x1, blocking collectives, on_device(): lax.all_gather(attended, 'head', axis=1, tiled=True)  10.7 us
    gather x5, local copies, waits for them, and re-layouts, allowed_keys(): key_seg = jnp.take(segments, clipped)  9.02 us
    dot_general x1, matrix products, on_device(): jnp.dot(lax.all_gather(attended, 'head', axis=1, tiled=True), out_weight,...  5.47 us
    dot_general x5, matrix products, absorb(): jnp.einsum('tagd,sad->agts', query_heads, key_heads, preferred_element_ty...  2.97 us
    dot_general x5, matrix products, absorb(): jnp.einsum('agts,sad->agtd', weights.astype(jnp.bfloat16), value_heads, p...  2.2 us
  transfers between devices with their start and end apart: 8, of which 0 were waited for; matrix products, arithmetic and copies ran while one was open for 28% of the time, Pallas kernels for 0%

commit v1 on v0

--- a/solution.py
+++ b/solution.py
@@ -91,7 +91,7 @@
     attended = (accum / row_sum[..., None]).transpose(2, 0, 1, 3)
     attended = attended.reshape(row_count, queries.shape[1]).astype(jnp.bfloat16)
     mixed = jnp.dot(
-        lax.all_gather(attended, "head", axis=1, tiled=True),
+        jnp.concatenate(lax.all_gather(attended, "head"), axis=1),
         out_weight,
         preferred_element_type=jnp.float32,
     )

time: 61.6 us -> 62 us (level)
  no operation moved by 1% of the time
where the time goes in v1:
time: 62 us; the launch traced here: 61.2 us
  starting transfers between devices  24.9 us (40%)
  local copies, waits for them, and re-layouts  11.5 us (19%)
  blocking collectives  10.7 us (17%)
  matrix products  10.6 us (17%)
  other arithmetic  2.91 us (5%)
    ppermute x8, starting transfers between devices, passed_along(): return lax.ppermute(block, axis, route)  24.9 us
    all_gather x1, blocking collectives, on_device(): lax.all_gather(attended, 'head')  10.7 us
    gather x5, local copies, waits for them, and re-layouts, allowed_keys(): key_seg = jnp.take(segments, clipped)  9.02 us
    dot_general x1, matrix products, on_device(): jnp.dot(jnp.concatenate(lax.all_gather(attended, 'head'), axis=1), out_we...  5.47 us
    dot_general x5, matrix products, absorb(): jnp.einsum('tagd,sad->agts', query_heads, key_heads, preferred_element_ty...  2.97 us
    dot_general x5, matrix products, absorb(): jnp.einsum('agts,sad->agtd', weights.astype(jnp.bfloat16), value_heads, p...  2.2 us
  transfers between devices with their start and end apart: 8, of which 0 were waited for; matrix products, arithmetic and copies ran while one was open for 28% of the time, Pallas kernels for 0%

profile of v1, /device:TPU:0, one launch (start us, length us, event | category | flops | bytes accessed | tf_op | source)
XLA Modules:
  0.0 61.2 jit_solution(8540363599064115750)
XLA Ops:
  0.0 2.4 %collective-permute-start.2 = (bf16[128,128]{1,0:T(8,128)(2,1)}, bf16[128,128]{1,0:T(8,128)(2,1)S(1)}, u32[]{:S(2)}, u32[]{:S(2)}) collective-permute-start(bf16[128,128]{1,0:T(8,128)(2,1)} %param.10), channel_id=1, source_target_pairs={{0,4},{4,8},{8,12},{12,16},{16,20},{20,24},{24,28},{1,5},{5,9},{9,... | collective-permute-start | bytes 98312 | tf_op jit(solution)/shard_map/ppermute | solution.py:14
  2.4 4.6 %collective-permute-start.3 = (bf16[128,128]{1,0:T(8,128)(2,1)}, bf16[128,128]{1,0:T(8,128)(2,1)S(1)}, u32[]{:S(2)}, u32[]{:S(2)}) collective-permute-start(bf16[128,128]{1,0:T(8,128)(2,1)} %param.11), channel_id=1, source_target_pairs={{0,4},{4,8},{8,12},{12,16},{16,20},{20,24},{24,28},{1,5},{5,9},{9,... | collective-permute-start | bytes 98312 | tf_op jit(solution)/shard_map/ppermute | solution.py:14
  7.1 0.8 %dynamic_slice.3 = s32[128]{0:T(128)S(1)} dynamic-slice(s32[1024]{0:T(1024)} %param.12, s32[]{:T(128)S(6)} %select_n.63), dynamic_slice_sizes={128} | dynamic-slice | bytes 1028 | tf_op jit(solution)/shard_map/dynamic_slice | solution.py:61
  7.8 1.6 %gather_fusion.2 = s32[128]{0:T(128)S(1)} fusion(s32[1024]{0:T(1024)} %param.12, s32[1024]{0:T(1024)S(1)} %pad_clamp_fusion.1), kind=kCustom, calls=%fused_computation.2.clone | custom fusion | bytes 1536 | tf_op jit(solution)/shard_map/jit(_take)/gather | solution.py:20
  9.5 1.6 %gather_fusion.1 = s32[128]{0:T(128)S(1)} fusion(s32[1024]{0:T(1024)} %param.12, s32[1024]{0:T(1024)S(1)} %pad_clamp_fusion.2), kind=kCustom, calls=%fused_computation.clone | custom fusion | bytes 1536 | tf_op jit(solution)/shard_map/jit(_take)/gather | solution.py:20
  11.1 0.2 fusion.40
  11.3 1.1 %fusion.54 = (f32[4,128]{1,0:T(4,128)S(1)}, f32[1,4,128,128]{2,3,1,0:T(8,128)S(1)}) fusion(bf16[128,128]{1,0:T(8,128)(2,1)} %param.10, pred[128,128]{0,1:T(8,128)(4,1)S(1)} %get-tuple-element.294, bf16[128,512]{1,0:T(8,128)(2,1)} %param.9), kind=kOutput, calls=%fused_computation.96 | convolution fusion | flops 16973312 | bytes 444416 | tf_op jit(solution)/shard_map/tagd,sad->agts/dot_general | solution.py:33
  12.4 1.0 %copy.24 = bf16[128,512]{0,1:T(8,128)(2,1)S(1)} copy(bf16[128,512]{1,0:T(8,128)(2,1)} %param.9) | data formatting | bytes 262144 | tf_op args[0]
  13.4 0.1 copy.25
  13.6 0.0 collective-permute-done.2
  13.6 1.1 %fusion.55 = (f32[4,128]{1,0:T(4,128)S(1)}, f32[1,4,128,128]{2,3,1,0:T(8,128)S(1)}) fusion(bf16[128,128]{1,0:T(8,128)(2,1)S(1)} %collective-permute-done.2, pred[128,128]{0,1:T(8,128)(4,1)S(1)} %get-tuple-element.295, bf16[128,512]{1,0:T(8,128)(2,1)} %param.9), kind=kOutput, calls=%fused_computation.97 | convolution fusion | flops 16973312 | bytes 444416 | tf_op jit(solution)/shard_map/tagd,sad->agts/dot_general | solution.py:33
  14.7 0.1 fusion.25
  14.8 1.0 %fusion.19 = f32[4,128,128]{2,1,0:T(8,128)S(1)} fusion(f32[1,4,128,128]{2,3,1,0:T(8,128)S(1)} %get-tuple-element.297, f32[4,128]{1,0:T(4,128)S(1)} %get-tuple-element.288, f32[4,128]{1,0:T(4,128)S(1)} %get-tuple-element.292, f32[4,128]{1,0:T(4,128)S(1)} %get-tuple-element.293, bf16[128,128]{1,0:T(8,128)(2,1)} %param.11), kind=kOutput, calls=%fused_computation.36 | convolution fusion | flops 17039360 | bytes 563200 | tf_op jit(solution)/shard_map/agts,sad->agtd/dot_general | solution.py:41
  15.8 0.1 fusion.27
  15.9 0.8 %pad_maximum_fusion = bf16[256,128]{1,0:T(8,128)(2,1)S(1)} fusion(bf16[128,128]{1,0:T(8,128)(2,1)} %param.10, bf16[128,128]{1,0:T(8,128)(2,1)S(1)} %collective-permute-done.2), kind=kLoop, calls=%fused_computation.58 | loop fusion | flops 131072 | bytes 131072 | tf_op jit(solution)/shard_map/concatenate | solution.py:78
  16.6 0.0 collective-permute-done.3
  16.6 0.8 %pad_maximum_fusion.1 = bf16[256,128]{1,0:T(8,128)(2,1)S(1)} fusion(bf16[128,128]{1,0:T(8,128)(2,1)} %param.11, bf16[128,128]{1,0:T(8,128)(2,1)S(1)} %collective-permute-done.3), kind=kLoop, calls=%fused_computation.59 | loop fusion | flops 131072 | bytes 131072 | tf_op jit(solution)/shard_map/concatenate | solution.py:79
  17.4 0.2 fusion.18
  17.6 26.8 %while.23 = (s32[]{:T(128)}, bf16[256,128]{1,0:T(8,128)(2,1)S(1)}, bf16[256,128]{1,0:T(8,128)(2,1)S(1)}, f32[1,4,128]{2,1,0:T(4,128)S(1)}, f32[1,4,128]{2,1,0:T(...) while((s32[]{:T(128)}, bf16[256,128]{1,0:T(8,128)(2,1)S(1)}, ...), condition=%wide.region_7.9_spmd.clone.clone, body=%wide.region_4.8_spmd.clone.clone.sunk | while | flops 68393600 | bytes 3260693 | solution.py:88
  17.6 3.5 %collective-permute-start = (bf16[256,128]{1,0:T(8,128)(2,1)S(1)}, bf16[256,128]{1,0:T(8,128)(2,1)S(1)}, u32[]{:S(2)}, u32[]{:S(2)}) collective-permute-start(bf16[256,128]{1,0:T(8,128)(2,1)S(1)} %get-tuple-element.394), channel_id=1, source_target_pairs={{0,8},{4,12},{8,16},{12,20},{16,24},{20,28},{1,9},{5,13},{9,17},{1... | collective-permute-start | bytes 196616 | tf_op jit(solution)/shard_map/while/body/eval_jaxpr/ppermute | solution.py:14
  21.1 3.5 %collective-permute-start.1 = (bf16[256,128]{1,0:T(8,128)(2,1)S(1)}, bf16[256,128]{1,0:T(8,128)(2,1)S(1)}, u32[]{:S(2)}, u32[]{:S(2)}) collective-permute-start(bf16[256,128]{1,0:T(8,128)(2,1)S(1)} %get-tuple-element.395), channel_id=1, source_target_pairs={{0,8},{4,12},{8,16},{12,20},{16,24},{20,28},{1,9},{5,13},{9,17},{1... | collective-permute-start | bytes 196616 | tf_op jit(solution)/shard_map/while/body/eval_jaxpr/ppermute | solution.py:14
  24.7 1.9 %gather_fusion = s32[256]{0:T(256)S(1)} fusion(s32[1024]{0:T(1024)} %get-tuple-element.414, s32[1024]{0:T(1024)S(1)} %pad_clamp_fusion.4), kind=kCustom, calls=%fused_computation.1.clone.clone.clone.1 | custom fusion | bytes 3072 | tf_op jit(solution)/shard_map/while/body/eval_jaxpr/jit(_take)/gather | solution.py:20
  26.6 0.2 fusion.71
  26.8 0.0 collective-permute-done
  26.8 0.2 fusion.72
  27.1 0.1 fusion.74
  27.3 0.3 fusion.75
  27.6 3.5 %collective-permute-start = (bf16[256,128]{1,0:T(8,128)(2,1)S(1)}, bf16[256,128]{1,0:T(8,128)(2,1)S(1)}, u32[]{:S(2)}, u32[]{:S(2)}) collective-permute-start(bf16[256,128]{1,0:T(8,128)(2,1)S(1)} %get-tuple-element.394), channel_id=1, source_target_pairs={{0,8},{4,12},{8,16},{12,20},{16,24},{20,28},{1,9},{5,13},{9,17},{1... | collective-permute-start | bytes 196616 | tf_op jit(solution)/shard_map/while/body/eval_jaxpr/ppermute | solution.py:14
  31.1 1.9 %collective-permute-start.1 = (bf16[256,128]{1,0:T(8,128)(2,1)S(1)}, bf16[256,128]{1,0:T(8,128)(2,1)S(1)}, u32[]{:S(2)}, u32[]{:S(2)}) collective-permute-start(bf16[256,128]{1,0:T(8,128)(2,1)S(1)} %get-tuple-element.395), channel_id=1, source_target_pairs={{0,8},{4,12},{8,16},{12,20},{16,24},{20,28},{1,9},{5,13},{9,17},{1... | collective-permute-start | bytes 196616 | tf_op jit(solution)/shard_map/while/body/eval_jaxpr/ppermute | solution.py:14
  33.1 1.9 %gather_fusion = s32[256]{0:T(256)S(1)} fusion(s32[1024]{0:T(1024)} %get-tuple-element.414, s32[1024]{0:T(1024)S(1)} %pad_clamp_fusion.4), kind=kCustom, calls=%fused_computation.1.clone.clone.clone.1 | custom fusion | bytes 3072 | tf_op jit(solution)/shard_map/while/body/eval_jaxpr/jit(_take)/gather | solution.py:20
  35.1 0.2 fusion.71
  35.3 0.2 fusion.72
  35.5 0.1 fusion.74
  35.7 0.3 fusion.75
  36.0 3.5 %collective-permute-start = (bf16[256,128]{1,0:T(8,128)(2,1)S(1)}, bf16[256,128]{1,0:T(8,128)(2,1)S(1)}, u32[]{:S(2)}, u32[]{:S(2)}) collective-permute-start(bf16[256,128]{1,0:T(8,128)(2,1)S(1)} %get-tuple-element.394), channel_id=1, source_target_pairs={{0,8},{4,12},{8,16},{12,20},{16,24},{20,28},{1,9},{5,13},{9,17},{1... | collective-permute-start | bytes 196616 | tf_op jit(solution)/shard_map/while/body/eval_jaxpr/ppermute | solution.py:14
  39.6 1.9 %collective-permute-start.1 = (bf16[256,128]{1,0:T(8,128)(2,1)S(1)}, bf16[256,128]{1,0:T(8,128)(2,1)S(1)}, u32[]{:S(2)}, u32[]{:S(2)}) collective-permute-start(bf16[256,128]{1,0:T(8,128)(2,1)S(1)} %get-tuple-element.395), channel_id=1, source_target_pairs={{0,8},{4,12},{8,16},{12,20},{16,24},{20,28},{1,9},{5,13},{9,17},{1... | collective-permute-start | bytes 196616 | tf_op jit(solution)/shard_map/while/body/eval_jaxpr/ppermute | solution.py:14
  41.6 1.9 %gather_fusion = s32[256]{0:T(256)S(1)} fusion(s32[1024]{0:T(1024)} %get-tuple-element.414, s32[1024]{0:T(1024)S(1)} %pad_clamp_fusion.4), kind=kCustom, calls=%fused_computation.1.clone.clone.clone.1 | custom fusion | bytes 3072 | tf_op jit(solution)/shard_map/while/body/eval_jaxpr/jit(_take)/gather | solution.py:20
  43.5 0.2 fusion.71
  43.7 0.0 collective-permute-done
  43.7 0.2 fusion.72
  44.0 0.1 fusion.74
  44.1 0.0 collective-permute-done.1
  44.1 0.3 fusion.75
  44.5 0.1 copy.26
  44.7 0.1 copy.27
  44.8 10.7 %all_gather.4 = bf16[4,128,512]{2,1,0:T(8,128)(2,1)S(1)} all-gather(bf16[1,128,512]{2,1,0:T(8,128)(2,1)S(1)} %copy.27), channel_id=1, replica_groups=mesh['seq'=8,'head'=4] {'head'}, dimensions={0}, use_global_device_ids=true | all-gather | bytes 655360 | tf_op jit(solution)/shard_map/all_gather | solution.py:94
  55.4 0.3 copy.28
  55.7 5.5 %convolution_convert_fusion = bf16[128,2048]{1,0:T(8,128)(2,1)} fusion(bf16[128,2048]{0,1:T(8,128)(2,1)S(1)} %bitcast.143, bf16[2048,2048]{1,0:T(8,128)(2,1)} %param.13), kind=kOutput, calls=%fused_computation.32 | convolution fusion | flops 1074003968 | bytes 9437184 | tf_op jit(solution)/shard_map/dot_general | solution.py:93
  (43 shorter events, 0.3 us)
Async XLA Ops:
  0.0 13.6 %collective-permute-start.2 = (bf16[128,128]{1,0:T(8,128)(2,1)}, bf16[128,128]{1,0:T(8,128)(2,1)S(1)}, u32[]{:S(2)}, u32[]{:S(2)}) collective-permute-start(bf16[128,128]{1,0:T(8,128)(2,1)} %param.10), channel_id=1, source_target_pairs={{0,4},{4,8},{8,12},{12,16},{16,20},{20,24},{24,28},{1,5},{5,9},{9,... | collective-permute-start | bytes 98312 | tf_op jit(solution)/shard_map/ppermute | solution.py:14
  2.4 14.2 %collective-permute-start.3 = (bf16[128,128]{1,0:T(8,128)(2,1)}, bf16[128,128]{1,0:T(8,128)(2,1)S(1)}, u32[]{:S(2)}, u32[]{:S(2)}) collective-permute-start(bf16[128,128]{1,0:T(8,128)(2,1)} %param.11), channel_id=1, source_target_pairs={{0,4},{4,8},{8,12},{12,16},{16,20},{20,24},{24,28},{1,5},{5,9},{9,... | collective-permute-start | bytes 98312 | tf_op jit(solution)/shard_map/ppermute | solution.py:14
  17.6 9.2 %collective-permute-start = (bf16[256,128]{1,0:T(8,128)(2,1)S(1)}, bf16[256,128]{1,0:T(8,128)(2,1)S(1)}, u32[]{:S(2)}, u32[]{:S(2)}) collective-permute-start(bf16[256,128]{1,0:T(8,128)(2,1)S(1)} %get-tuple-element.394), channel_id=1, source_target_pairs={{0,8},{4,12},{8,16},{12,20},{16,24},{20,28},{1,9},{5,13},{9,17},{1... | collective-permute-start | bytes 196616 | tf_op jit(solution)/shard_map/while/body/eval_jaxpr/ppermute | solution.py:14
  21.1 6.1 %collective-permute-start.1 = (bf16[256,128]{1,0:T(8,128)(2,1)S(1)}, bf16[256,128]{1,0:T(8,128)(2,1)S(1)}, u32[]{:S(2)}, u32[]{:S(2)}) collective-permute-start(bf16[256,128]{1,0:T(8,128)(2,1)S(1)} %get-tuple-element.395), channel_id=1, source_target_pairs={{0,8},{4,12},{8,16},{12,20},{16,24},{20,28},{1,9},{5,13},{9,17},{1... | collective-permute-start | bytes 196616 | tf_op jit(solution)/shard_map/while/body/eval_jaxpr/ppermute | solution.py:14
  27.6 7.7 %collective-permute-start = (bf16[256,128]{1,0:T(8,128)(2,1)S(1)}, bf16[256,128]{1,0:T(8,128)(2,1)S(1)}, u32[]{:S(2)}, u32[]{:S(2)}) collective-permute-start(bf16[256,128]{1,0:T(8,128)(2,1)S(1)} %get-tuple-element.394), channel_id=1, source_target_pairs={{0,8},{4,12},{8,16},{12,20},{16,24},{20,28},{1,9},{5,13},{9,17},{1... | collective-permute-start | bytes 196616 | tf_op jit(solution)/shard_map/while/body/eval_jaxpr/ppermute | solution.py:14
  31.1 4.5 %collective-permute-start.1 = (bf16[256,128]{1,0:T(8,128)(2,1)S(1)}, bf16[256,128]{1,0:T(8,128)(2,1)S(1)}, u32[]{:S(2)}, u32[]{:S(2)}) collective-permute-start(bf16[256,128]{1,0:T(8,128)(2,1)S(1)} %get-tuple-element.395), channel_id=1, source_target_pairs={{0,8},{4,12},{8,16},{12,20},{16,24},{20,28},{1,9},{5,13},{9,17},{1... | collective-permute-start | bytes 196616 | tf_op jit(solution)/shard_map/while/body/eval_jaxpr/ppermute | solution.py:14
  36.0 7.7 %collective-permute-start = (bf16[256,128]{1,0:T(8,128)(2,1)S(1)}, bf16[256,128]{1,0:T(8,128)(2,1)S(1)}, u32[]{:S(2)}, u32[]{:S(2)}) collective-permute-start(bf16[256,128]{1,0:T(8,128)(2,1)S(1)} %get-tuple-element.394), channel_id=1, source_target_pairs={{0,8},{4,12},{8,16},{12,20},{16,24},{20,28},{1,9},{5,13},{9,17},{1... | collective-permute-start | bytes 196616 | tf_op jit(solution)/shard_map/while/body/eval_jaxpr/ppermute | solution.py:14
  39.6 4.6 %collective-permute-start.1 = (bf16[256,128]{1,0:T(8,128)(2,1)S(1)}, bf16[256,128]{1,0:T(8,128)(2,1)S(1)}, u32[]{:S(2)}, u32[]{:S(2)}) collective-permute-start(bf16[256,128]{1,0:T(8,128)(2,1)S(1)} %get-tuple-element.395), channel_id=1, source_target_pairs={{0,8},{4,12},{8,16},{12,20},{16,24},{20,28},{1,9},{5,13},{9,17},{1... | collective-permute-start | bytes 196616 | tf_op jit(solution)/shard_map/while/body/eval_jaxpr/ppermute | solution.py:14
